TPU v7x, 32 devices: a whole 2x2x4 slice. The times are simulated.
32 devices in a mesh: gx: 2 (over y), gy: 4 (over z), gz: 4 (over x, core).
Axes of the slice: x: 2, y: 2, z: 4, core: 2. Of those that a mesh axis runs over, the one named last changes fastest.
Arguments:
- kappa_sq: float32 [32, 64, 512], P('gx', 'gz', 'gy'), may hold values from 0.004 to 0.4
- probe_bits: int32 [4, 32, 64, 512], P(None, 'gx', 'gz', 'gy'), may hold values from 0 to 1
Outputs:
- solution: float32 [4, 32, 64, 512], P(None, 'gx', 'gz', 'gy')
- relative_residual: float32 [4], replicated
All inputs are finite; a program needn't handle non-finite values.
Results may differ from a plain program's by a relative error of at most 0.0001.
Values sent between devices are 32-bit elements; how exact they have to be, the bound alone decides.
A program may use at most 128 MiB of HBM per device.

v0:
```python
import jax
import jax.numpy as jnp
from jax import lax
from jax.sharding import PartitionSpec as P

LEVELS = 3
COARSE_SWEEPS = 8
ITERS = 2
damping = 0.8


def extended(block, sides, width):
    for axis, dim in sides:
        count = lax.axis_size(axis)
        forward = [(i, i + 1) for i in range(count - 1)]
        backward = [(target, source) for source, target in forward]
        low = lax.ppermute(
            lax.slice_in_dim(block, block.shape[dim] - width, None, axis=dim), axis, forward
        )
        high = lax.ppermute(lax.slice_in_dim(block, 0, width, axis=dim), axis, backward)
        block = jnp.concatenate([low, block, high], axis=dim)
    return block


def neighbours(padded):
    along_first = padded[..., 2:, 1:-1, 1:-1] + padded[..., :-2, 1:-1, 1:-1]
    along_second = padded[..., 1:-1, 2:, 1:-1] + padded[..., 1:-1, :-2, 1:-1]
    along_third = padded[..., 1:-1, 1:-1, 2:] + padded[..., 1:-1, 1:-1, :-2]
    return along_first + along_second + along_third


def coarsen(field):
    leading = field.shape[:-3]
    cells_first, cells_second, cells_third = field.shape[-3:]
    grouped = field.reshape(
        leading + (cells_first // 2, 2, cells_second // 2, 2, cells_third // 2, 2)
    )
    return jnp.mean(grouped, axis=(-5, -3, -1))


def refine(field):
    leading = field.shape[:-3]
    cells_first, cells_second, cells_third = field.shape[-3:]
    spread = field.reshape(leading + (cells_first, 1, cells_second, 1, cells_third, 1))
    spread = jnp.broadcast_to(spread, leading + (cells_first, 2, cells_second, 2, cells_third, 2))
    return spread.reshape(leading + (cells_first * 2, cells_second * 2, cells_third * 2))


def level_faces(field, grid_level):
    if grid_level == 0:
        return extended(field, (("gx", 1), ("gy", 3), ("gz", 2)), 1)
    return extended(field, (("gx", 1), ("gy", 3), ("gz", 2)), 1)


def operate(field, diagonal, coupling, grid_level):
    return diagonal * field - coupling * neighbours(level_faces(field, grid_level))


def jacobi_sweep(field, rhs_field, diagonal, coupling, grid_level):
    return field + damping * (rhs_field - operate(field, diagonal, coupling, grid_level)) / diagonal


def assemble(gathered):
    count_x = lax.axis_size("gx")
    count_y = lax.axis_size("gy")
    count_z = lax.axis_size("gz")
    leading = gathered.shape[1:-3]
    cells_first, cells_second, cells_third = gathered.shape[-3:]
    lead_count = len(leading)
    blocks = gathered.reshape(
        (count_x, count_y, count_z) + leading + (cells_first, cells_second, cells_third)
    )
    permutation = tuple(range(3, 3 + lead_count)) + (
        0,
        3 + lead_count,
        2,
        4 + lead_count,
        1,
        5 + lead_count,
    )
    blocks = jnp.transpose(blocks, permutation)
    return blocks.reshape(
        leading + (count_x * cells_first, count_z * cells_second, count_y * cells_third)
    )


def local_dot(first_field, second_field):
    return jnp.sum(first_field * second_field, axis=(1, 2, 3))


def expand(values):
    return values[:, None, None, None]


def per_device(kappa_sq, probe_bits):
    diagonals = []
    couplings = []
    coef_field = kappa_sq
    for grid_level in range(LEVELS + 1):
        if grid_level > 0:
            coef_field = coarsen(coef_field)
        coupling = 0.25**grid_level
        diagonals.append(coef_field + 6.0 * coupling)
        couplings.append(coupling)
    global_diag = assemble(
        lax.all_gather(diagonals[LEVELS][None], ("gx", "gy", "gz"), axis=0, tiled=True)
    )

    def coarsest(rhs_field):
        diagonal = diagonals[LEVELS]
        coupling = couplings[LEVELS]
        global_rhs = assemble(
            lax.all_gather(rhs_field[None], ("gx", "gy", "gz"), axis=0, tiled=True)
        )
        field = damping * global_rhs / global_diag
        for sweep_index in range(COARSE_SWEEPS - 1):
            padded = jnp.pad(field, ((0, 0), (1, 1), (1, 1), (1, 1)))
            field = (
                field
                + damping
                * (global_rhs - (global_diag * field - coupling * neighbours(padded)))
                / global_diag
            )
        probes, block_x, block_z, block_y = rhs_field.shape
        zero_index = jnp.zeros((), jnp.int32)
        starts = (
            zero_index,
            lax.axis_index("gx") * block_x,
            lax.axis_index("gz") * block_z,
            lax.axis_index("gy") * block_y,
        )
        return lax.dynamic_slice(field, starts, (probes, block_x, block_z, block_y))

    def vcycle(rhs_field, grid_level):
        if grid_level == LEVELS:
            return coarsest(rhs_field)
        diagonal = diagonals[grid_level]
        coupling = couplings[grid_level]
        field = damping * rhs_field / diagonal
        field = jacobi_sweep(field, rhs_field, diagonal, coupling, grid_level)
        remainder = rhs_field - operate(field, diagonal, coupling, grid_level)
        field = field + refine(vcycle(coarsen(remainder), grid_level + 1))
        field = jacobi_sweep(field, rhs_field, diagonal, coupling, grid_level)
        return jacobi_sweep(field, rhs_field, diagonal, coupling, grid_level)

    right_side = 2.0 * probe_bits.astype(jnp.float32) - 1.0
    solution = jnp.zeros_like(right_side)
    residual = right_side
    fine_diag = diagonals[0]

    def precond_sum(first_field, second_field):
        return lax.psum(local_dot(first_field, second_field), ("gx", "gy", "gz"))

    precond = vcycle(residual, 0)
    precond_dot = precond_sum(residual, precond)
    search = precond
    for iteration in range(ITERS):
        operated = operate(search, fine_diag, 1.0, 0)
        step_size = precond_dot / lax.psum(local_dot(search, operated), ("gx", "gy", "gz"))
        solution = solution + expand(step_size) * search
        residual = residual - expand(step_size) * operated
        if iteration + 1 < ITERS:
            precond = vcycle(residual, 0)
            next_dot = precond_sum(residual, precond)
            search = precond + expand(next_dot / precond_dot) * search
            precond_dot = next_dot
    squares = lax.psum(local_dot(residual, residual), ("gx", "gy", "gz"))
    cell_total = (
        probe_bits.shape[1]
        * probe_bits.shape[2]
        * probe_bits.shape[3]
        * lax.axis_size("gx")
        * lax.axis_size("gy")
        * lax.axis_size("gz")
    )
    return (solution, jnp.sqrt(squares / cell_total))


def solution(mesh):
    return jax.shard_map(
        per_device,
        mesh=mesh,
        in_specs=(P("gx", "gz", "gy"), P(None, "gx", "gz", "gy")),
        out_specs=(P(None, "gx", "gz", "gy"), P()),
        check_vma=False,
    )
```

profile of v0, /device:TPU:0, one launch (start us, length us, event | category | flops | bytes accessed | tf_op | source)
XLA Modules:
  0.0 1080.8 jit_solution(16804115378510842129)
XLA Ops:
  2.7 4.9 collective-permute-start.1
  16.0 4.5 collective-permute-start.2
  40.4 4.8 collective-permute-start.8
  45.2 9.7 reshape.124
  69.1 8.8 copy.1882
  77.9 11.7 %reduce_sum.126 = f32[4,8,8,64]{0,3,2,1:T(8,128)S(1)} reduce(f32[4,8,2,8,2,64,2]{0,6,5,4,3,2,1:T(2,128)} %bitcast.21, f32[]{:T(128)} %constant.28.clone.1), dimensions={2,4,6}, to_apply=%region_0.0 | reduce | flops 114688 | bytes 589828 | tf_op jit(solution)/shard_map/reduce_sum | solution.py:38
  99.1 4.6 collective-permute-start.14
  117.1 4.3 collective-permute-done.18
  122.8 4.7 collective-permute-start.20
  147.8 4.4 collective-permute-start.26
  154.1 4.4 collective-permute-done.27
  168.1 47.4 %all-gather.1 = f32[64,2,16]{2,1,0:T(2,128)S(1)} all-gather(f32[2,2,16]{2,1,0:T(2,128)S(1)} %multiply_add_fusion.3), channel_id=3, replica_groups=mesh['gx'=2,'gy'=4,'gz'=4] {'gx','gy','gz'}, dimensions={0}, use_global_device_ids=true | all-gather | bytes 8448 | tf_op jit(solution)/shard_map/all_gather | solution.py:106
  230.6 40.5 %all-gather = f32[128,2,2,16]{3,2,1,0:T(2,128)S(1)} all-gather(f32[4,2,2,16]{3,2,1,0:T(2,128)S(1)} %copy.1905), channel_id=2, replica_groups=mesh['gx'=2,'gy'=4,'gz'=4] {'gx','gy','gz'}, dimensions={0}, use_global_device_ids=true | all-gather | bytes 33792 | tf_op jit(solution)/shard_map/all_gather | solution.py:113
  283.4 4.3 collective-permute-done.39
  298.5 4.3 collective-permute-done.42
  306.0 4.3 collective-permute-done.45
  328.2 4.6 collective-permute-start.50
  337.1 4.6 collective-permute-start.53
  351.9 4.7 collective-permute-start.56
  361.0 5.0 collective-permute-start.59
  369.5 7.8 broadcast_in_dim.14
  377.3 10.0 copy.1931
  397.7 4.7 collective-permute-start.62
  405.1 4.3 collective-permute-start.65
  410.8 5.8 collective-permute-done.64
  427.6 4.8 collective-permute-start.68
  453.6 4.8 collective-permute-start.74
  469.7 41.7 %all-reduce.14 = (f32[4]{0:T(128)S(1)}, f32[4]{0:T(128)S(1)}) all-reduce(f32[4]{0:T(128)S(1)} %get-tuple-element.13, f32[4]{0:T(128)S(1)} %get-tuple-element.12), channel_id=1, replica_groups=mesh['gx'=2,'gy'=4,'gz'=4] {'gx','gy','gz'}, use_global_device_ids=true, to_apply=%region_7.8 | all-reduce | flops 8 | bytes 64 | tf_op jit(solution)/shard_map/psum | solution.py:152
  524.4 4.5 collective-permute-start.80
  550.0 4.8 collective-permute-start.86
  566.8 8.8 copy.1982
  575.7 13.1 %reduce_sum.134 = f32[4,8,8,64]{0,3,2,1:T(8,128)} reduce(f32[4,8,2,8,2,64,2]{0,6,5,4,3,2,1:T(2,128)} %bitcast.23, f32[]{:T(128)} %constant.28.clone.1), dimensions={2,4,6}, to_apply=%region_10.11 | reduce | flops 114688 | bytes 589828 | tf_op jit(solution)/shard_map/reduce_sum | solution.py:38
  599.8 4.9 collective-permute-start.92
  623.4 4.7 collective-permute-start.98
  652.0 4.4 collective-permute-start.104
  658.3 4.4 collective-permute-done.105
  701.8 44.2 %all-gather.2 = f32[128,2,2,16]{3,2,1,0:T(2,128)S(1)} all-gather(f32[4,2,2,16]{3,2,1,0:T(2,128)S(1)} %copy.2005), channel_id=4, replica_groups=mesh['gx'=2,'gy'=4,'gz'=4] {'gx','gy','gz'}, dimensions={0}, use_global_device_ids=true | all-gather | bytes 33792 | tf_op jit(solution)/shard_map/all_gather | solution.py:113
  815.0 4.6 collective-permute-start.128
  836.9 5.0 collective-permute-start.134
  853.7 8.9 broadcast_in_dim.17
  862.6 10.0 copy.2029
  883.0 5.0 collective-permute-start.140
  893.9 5.8 collective-permute-done.142
  910.7 5.1 collective-permute-start.146
  926.9 41.6 %psum.37 = f32[4]{0:T(128)S(1)} all-reduce(f32[4]{0:T(128)S(1)} %get-tuple-element.18), channel_id=1, replica_groups=mesh['gx'=2,'gy'=4,'gz'=4] {'gx','gy','gz'}, use_global_device_ids=true, to_apply=%region_14.15 | all-reduce | flops 4 | bytes 32 | tf_op jit(solution)/shard_map/psum | solution.py:152
  981.2 4.5 collective-permute-start.152
  996.1 41.6 %psum.38 = f32[4]{0:T(128)S(1)} all-reduce(f32[4]{0:T(128)S(1)} %get-tuple-element.16), channel_id=1, replica_groups=mesh['gx'=2,'gy'=4,'gz'=4] {'gx','gy','gz'}, use_global_device_ids=true, to_apply=%region_16.17 | all-reduce | flops 4 | bytes 32 | tf_op jit(solution)/shard_map/psum | solution.py:159
  1038.8 41.2 %psum.39 = f32[4]{0:T(128)S(1)} all-reduce(f32[4]{0:T(128)S(1)} %get-tuple-element.199), channel_id=1, replica_groups=mesh['gx'=2,'gy'=4,'gz'=4] {'gx','gy','gz'}, use_global_device_ids=true, to_apply=%region_18.19 | all-reduce | flops 4 | bytes 32 | tf_op jit(solution)/shard_map/psum | solution.py:167
  (671 shorter events, 539.1 us)
Async XLA Ops:
  2.7 6.5 collective-permute-start.1
  14.2 6.3 collective-permute-start.3
  38.6 20.4 %collective-permute-start.9 = (f32[4,18,16,1]{1,2,3,0:T(8,128)S(1)}, f32[4,18,16,1]{1,2,3,0:T(8,128)S(1)}, u32[]{:S(2)}, u32[]{:S(2)}) collective-permute-start(f32[4,18,16,1]{1,2,3,0:T(8,128)S(1)} %copy.1873), channel_id=1, source_target_pairs={{4,0},{8,4},{12,8},{5,1},{9,5},{13,9},{6,2},{10,6},{14,10},{7,3},{... | collective-permute-start | bytes 13832 | tf_op jit(solution)/shard_map/ppermute | solution.py:20
  40.4 19.1 %collective-permute-start.8 = (f32[4,18,16,1]{1,2,3,0:T(8,128)S(1)}, f32[4,18,16,1]{1,2,3,0:T(8,128)S(1)}, u32[]{:S(2)}, u32[]{:S(2)}) collective-permute-start(f32[4,18,16,1]{1,2,3,0:T(8,128)S(1)} %copy.1872), channel_id=1, source_target_pairs={{0,4},{4,8},{8,12},{1,5},{5,9},{9,13},{2,6},{6,10},{10,14},{3,7},{... | collective-permute-start | bytes 13832 | tf_op jit(solution)/shard_map/ppermute | solution.py:17
  97.8 8.1 collective-permute-start.15
  99.1 8.5 collective-permute-start.14
  121.5 8.8 collective-permute-start.21
  122.8 8.7 collective-permute-start.20
  147.8 6.3 collective-permute-start.26
  152.2 6.3 collective-permute-start.27
  165.2 50.5 %collective-permute-start.31 = (f32[4,1,4,32]{0,3,2,1:T(8,128)S(1)}, f32[4,1,4,32]{0,3,2,1:T(8,128)S(1)}, u32[]{:S(2)}, u32[]{:S(2)}) collective-permute-start(f32[4,1,4,32]{0,3,2,1:T(8,128)S(1)} %get-tuple-element.127), channel_id=1, source_target_pairs={{0,16},{1,17},{2,18},{3,19},{4,20},{5,21},{6,22},{7,23},{8,24},{9,... | collective-permute-start | bytes 6152 | tf_op jit(solution)/shard_map/ppermute | solution.py:17
  166.8 49.0 %collective-permute-start.30 = (f32[4,1,4,32]{0,3,2,1:T(8,128)S(1)}, f32[4,1,4,32]{0,3,2,1:T(8,128)S(1)}, u32[]{:S(2)}, u32[]{:S(2)}) collective-permute-start(f32[4,1,4,32]{0,3,2,1:T(8,128)S(1)} %get-tuple-element.128), channel_id=1, source_target_pairs={{16,0},{17,1},{18,2},{19,3},{20,4},{21,5},{22,6},{23,7},{24,8},{25... | collective-permute-start | bytes 6152 | tf_op jit(solution)/shard_map/ppermute | solution.py:20
  296.0 6.7 collective-permute-start.42
  326.9 7.2 collective-permute-start.51
  328.2 7.4 collective-permute-start.50
  350.6 7.4 collective-permute-start.57
  351.9 7.5 collective-permute-start.56
  359.7 6.3 collective-permute-start.58
  395.9 6.5 collective-permute-start.63
  397.7 6.3 collective-permute-start.62
  409.4 7.2 collective-permute-start.64
  425.8 6.6 collective-permute-start.69
  427.6 6.4 collective-permute-start.68
  451.8 6.6 collective-permute-start.75
  453.6 6.4 collective-permute-start.74
  522.6 6.3 collective-permute-start.81
  548.2 6.6 collective-permute-start.87
  550.0 6.4 collective-permute-start.86
  598.5 8.4 collective-permute-start.93
  599.8 8.8 collective-permute-start.92
  622.1 8.8 collective-permute-start.99
  623.4 8.7 collective-permute-start.98
  652.0 6.3 collective-permute-start.104
  656.4 6.3 collective-permute-start.105
  663.8 6.9 collective-permute-start.106
  766.3 7.0 collective-permute-start.118
  767.6 6.4 collective-permute-start.119
  792.7 6.9 collective-permute-start.124
  813.7 7.2 collective-permute-start.129
  815.0 7.4 collective-permute-start.128
  835.6 9.1 collective-permute-start.135
  836.9 8.9 collective-permute-start.134
  881.2 6.8 collective-permute-start.141
  883.0 6.6 collective-permute-start.140
  892.5 7.2 collective-permute-start.142
  908.9 6.8 collective-permute-start.147
  910.7 6.4 collective-permute-start.146
  979.4 6.3 collective-permute-start.153
  (128 other events, 821.3 us)
where the time goes:
time: 1090 us; the launch traced here: 1080 us
  starting transfers between devices  340 us (31%)
  blocking collectives  298 us (27%)
  waiting for transfers between devices  234 us (21%)
  local copies, waits for them, and re-layouts  131 us (12%)
  other arithmetic  74.1 us (7%)
    ppermute x78, starting transfers between devices, extended(): lax.ppermute(lax.slice_in_dim(block, block.shape[dim] - width, None, axis...  238 us
    ppermute x78, waiting for transfers between devices, extended(): lax.ppermute(lax.slice_in_dim(block, 0, width, axis=dim), axis, backward)  195 us
    ppermute x78, starting transfers between devices, extended(): lax.ppermute(lax.slice_in_dim(block, 0, width, axis=dim), axis, backward)  101 us
    all_gather x2, blocking collectives, coarsest(): lax.all_gather(rhs_field[None], ('gx', 'gy', 'gz'), axis=0, tiled=True)  84.7 us
    psum x2, blocking collectives, precond_sum(): return lax.psum(local_dot(first_field, second_field), ('gx', 'gy', 'gz'))  83.3 us
    all_gather x1, blocking collectives, per_device(): lax.all_gather(diagonals[LEVELS][None], ('gx', 'gy', 'gz'), axis=0, tiled...  47.4 us
    psum x1, blocking collectives, per_device(): lax.psum(local_dot(search, operated), ('gx', 'gy', 'gz'))  41.6 us
    psum x1, blocking collectives, per_device(): squares = lax.psum(local_dot(residual, residual), ('gx', 'gy', 'gz'))  41.2 us
  transfers between devices with their start and end apart: 156, of which 111 were waited for; matrix products, arithmetic and copies ran while one was open for 3% of the time, Pallas kernels for 0%

commit v1 on v0

--- a/solution.py
+++ b/solution.py
@@ -149,7 +149,7 @@
     fine_diag = diagonals[0]
 
     def precond_sum(first_field, second_field):
-        return lax.psum(local_dot(first_field, second_field), ("gx", "gy", "gz"))
+        return lax.psum(lax.psum(local_dot(first_field, second_field), ("gy", "gz")), "gx")
 
     precond = vcycle(residual, 0)
     precond_dot = precond_sum(residual, precond)

time: 1090 us -> 1120 us (1.028)
  blocking collectives: 298 us -> 326 us
    psum x1 -> x2, blocking collectives: 41.6 us -> 76.8 us  [per_device(): lax.psum(local_dot(search, operated), ('gx', 'gy', 'gz'))]
    psum x2 -> x4, blocking collectives: 83.3 us -> 78.6 us  [the longest x2 68.5 us: precond_sum(): lax.psum(local_dot(first_field, second_field), ('gy', 'gz'))]
where the time goes in v1:
time: 1120 us; the launch traced here: 1100 us
  starting transfers between devices  338 us (30%)
  blocking collectives  326 us (29%)
  waiting for transfers between devices  230 us (21%)
  local copies, waits for them, and re-layouts  131 us (12%)
  other arithmetic  74 us (7%)
    ppermute x78, starting transfers between devices, extended(): lax.ppermute(lax.slice_in_dim(block, block.shape[dim] - width, None, axis...  237 us
    ppermute x78, waiting for transfers between devices, extended(): lax.ppermute(lax.slice_in_dim(block, 0, width, axis=dim), axis, backward)  191 us
    ppermute x78, starting transfers between devices, extended(): lax.ppermute(lax.slice_in_dim(block, 0, width, axis=dim), axis, backward)  101 us
    all_gather x2, blocking collectives, coarsest(): lax.all_gather(rhs_field[None], ('gx', 'gy', 'gz'), axis=0, tiled=True)  84.7 us
    psum x2, blocking collectives, per_device(): lax.psum(local_dot(search, operated), ('gx', 'gy', 'gz'))  76.8 us
    psum x2, blocking collectives, precond_sum(): lax.psum(local_dot(first_field, second_field), ('gy', 'gz'))  68.5 us
    all_gather x1, blocking collectives, per_device(): lax.all_gather(diagonals[LEVELS][None], ('gx', 'gy', 'gz'), axis=0, tiled...  47.4 us
    ppermute x78, waiting for transfers between devices, extended(): lax.ppermute(lax.slice_in_dim(block, block.shape[dim] - width, None, axis...  39.3 us
  transfers between devices with their start and end apart: 156, of which 111 were waited for; matrix products, arithmetic and copies ran while one was open for 3% of the time, Pallas kernels for 0%

profile of v1, /device:TPU:0, one launch (start us, length us, event | category | flops | bytes accessed | tf_op | source)
XLA Modules:
  0.0 1102.3 jit_solution(16106617621000621389)
XLA Ops:
  2.7 4.9 collective-permute-start.1
  16.0 4.5 collective-permute-start.2
  40.4 4.8 collective-permute-start.8
  45.2 9.7 reshape.124
  69.1 8.8 copy.1882
  77.9 11.7 %reduce_sum.126 = f32[4,8,8,64]{0,3,2,1:T(8,128)S(1)} reduce(f32[4,8,2,8,2,64,2]{0,6,5,4,3,2,1:T(2,128)} %bitcast.21, f32[]{:T(128)} %constant.28.clone.1), dimensions={2,4,6}, to_apply=%region_0.0 | reduce | flops 114688 | bytes 589828 | tf_op jit(solution)/shard_map/reduce_sum | solution.py:38
  99.1 4.6 collective-permute-start.14
  117.1 4.3 collective-permute-done.18
  122.8 4.7 collective-permute-start.20
  147.8 4.4 collective-permute-start.26
  154.1 4.4 collective-permute-done.27
  168.1 47.4 %all-gather.1 = f32[64,2,16]{2,1,0:T(2,128)S(1)} all-gather(f32[2,2,16]{2,1,0:T(2,128)S(1)} %multiply_add_fusion.3), channel_id=3, replica_groups=mesh['gx'=2,'gy'=4,'gz'=4] {'gx','gy','gz'}, dimensions={0}, use_global_device_ids=true | all-gather | bytes 8448 | tf_op jit(solution)/shard_map/all_gather | solution.py:106
  230.6 40.6 %all-gather = f32[128,2,2,16]{3,2,1,0:T(2,128)S(1)} all-gather(f32[4,2,2,16]{3,2,1,0:T(2,128)S(1)} %copy.1905), channel_id=2, replica_groups=mesh['gx'=2,'gy'=4,'gz'=4] {'gx','gy','gz'}, dimensions={0}, use_global_device_ids=true | all-gather | bytes 33792 | tf_op jit(solution)/shard_map/all_gather | solution.py:113
  328.2 4.6 collective-permute-start.50
  337.1 4.6 collective-permute-start.53
  351.9 4.7 collective-permute-start.56
  361.0 5.0 collective-permute-start.59
  369.5 7.8 broadcast_in_dim.14
  377.3 10.0 copy.1931
  397.7 4.7 collective-permute-start.62
  405.1 4.3 collective-permute-start.65
  410.8 5.8 collective-permute-done.64
  427.6 4.8 collective-permute-start.68
  453.6 4.8 collective-permute-start.74
  469.7 34.3 %psum.49 = f32[4]{0:T(128)S(1)} all-reduce(f32[4]{0:T(128)S(1)} %get-tuple-element.13), channel_id=1, replica_groups=mesh['gx'=2,'gy'=4,'gz'=4] {'gy','gz'}, use_global_device_ids=true, to_apply=%region_7.8 | all-reduce | flops 4 | bytes 32 | tf_op jit(solution)/shard_map/psum | solution.py:152
  504.0 36.8 %psum.51 = f32[4]{0:T(128)S(1)} all-reduce(f32[4]{0:T(128)S(1)} %get-tuple-element.12), channel_id=1, replica_groups=mesh['gx'=2,'gy'=4,'gz'=4] {'gx','gy','gz'}, use_global_device_ids=true, to_apply=%region_10.11 | all-reduce | flops 4 | bytes 32 | tf_op jit(solution)/shard_map/psum | solution.py:159
  540.8 5.1 psum.50
  558.7 5.4 collective-permute-start.80
  583.4 4.8 collective-permute-start.86
  600.2 8.8 copy.1982
  609.0 13.1 %reduce_sum.134 = f32[4,8,8,64]{0,3,2,1:T(8,128)} reduce(f32[4,8,2,8,2,64,2]{0,6,5,4,3,2,1:T(2,128)} %bitcast.23, f32[]{:T(128)} %constant.28.clone.1), dimensions={2,4,6}, to_apply=%region_11.12 | reduce | flops 114688 | bytes 589828 | tf_op jit(solution)/shard_map/reduce_sum | solution.py:38
  633.1 4.9 collective-permute-start.92
  656.7 4.7 collective-permute-start.98
  685.3 4.4 collective-permute-start.104
  691.6 4.4 collective-permute-done.105
  735.1 44.2 %all-gather.2 = f32[128,2,2,16]{3,2,1,0:T(2,128)S(1)} all-gather(f32[4,2,2,16]{3,2,1,0:T(2,128)S(1)} %copy.2005), channel_id=4, replica_groups=mesh['gx'=2,'gy'=4,'gz'=4] {'gx','gy','gz'}, dimensions={0}, use_global_device_ids=true | all-gather | bytes 33792 | tf_op jit(solution)/shard_map/all_gather | solution.py:113
  848.2 4.6 collective-permute-start.128
  870.1 5.0 collective-permute-start.134
  886.9 8.9 broadcast_in_dim.17
  895.8 10.0 copy.2029
  916.2 5.0 collective-permute-start.140
  927.1 5.8 collective-permute-done.142
  944.0 5.1 collective-permute-start.146
  960.1 34.3 %psum.52 = f32[4]{0:T(128)S(1)} all-reduce(f32[4]{0:T(128)S(1)} %get-tuple-element.16), channel_id=1, replica_groups=mesh['gx'=2,'gy'=4,'gz'=4] {'gy','gz'}, use_global_device_ids=true, to_apply=%region_15.16 | all-reduce | flops 4 | bytes 32 | tf_op jit(solution)/shard_map/psum | solution.py:152
  994.4 4.9 psum.53
  1009.7 4.5 collective-permute-start.152
  1022.4 40.0 %psum.54 = f32[4]{0:T(128)S(1)} all-reduce(f32[4]{0:T(128)S(1)} %get-tuple-element.14), channel_id=1, replica_groups=mesh['gx'=2,'gy'=4,'gz'=4] {'gx','gy','gz'}, use_global_device_ids=true, to_apply=%region_18.19 | all-reduce | flops 4 | bytes 32 | tf_op jit(solution)/shard_map/psum | solution.py:159
  1063.4 38.1 %psum.55 = f32[4]{0:T(128)S(1)} all-reduce(f32[4]{0:T(128)S(1)} %get-tuple-element.197), channel_id=1, replica_groups=mesh['gx'=2,'gy'=4,'gz'=4] {'gx','gy','gz'}, use_global_device_ids=true, to_apply=%region_20.21 | all-reduce | flops 4 | bytes 32 | tf_op jit(solution)/shard_map/psum | solution.py:167
  (674 shorter events, 545.2 us)
Async XLA Ops:
  2.7 6.5 collective-permute-start.1
  14.2 6.3 collective-permute-start.3
  38.6 20.4 %collective-permute-start.9 = (f32[4,18,16,1]{1,2,3,0:T(8,128)S(1)}, f32[4,18,16,1]{1,2,3,0:T(8,128)S(1)}, u32[]{:S(2)}, u32[]{:S(2)}) collective-permute-start(f32[4,18,16,1]{1,2,3,0:T(8,128)S(1)} %copy.1873), channel_id=1, source_target_pairs={{4,0},{8,4},{12,8},{5,1},{9,5},{13,9},{6,2},{10,6},{14,10},{7,3},{... | collective-permute-start | bytes 13832 | tf_op jit(solution)/shard_map/ppermute | solution.py:20
  40.4 19.1 %collective-permute-start.8 = (f32[4,18,16,1]{1,2,3,0:T(8,128)S(1)}, f32[4,18,16,1]{1,2,3,0:T(8,128)S(1)}, u32[]{:S(2)}, u32[]{:S(2)}) collective-permute-start(f32[4,18,16,1]{1,2,3,0:T(8,128)S(1)} %copy.1872), channel_id=1, source_target_pairs={{0,4},{4,8},{8,12},{1,5},{5,9},{9,13},{2,6},{6,10},{10,14},{3,7},{... | collective-permute-start | bytes 13832 | tf_op jit(solution)/shard_map/ppermute | solution.py:17
  97.8 8.1 collective-permute-start.15
  99.1 8.5 collective-permute-start.14
  121.5 8.8 collective-permute-start.21
  122.8 8.7 collective-permute-start.20
  147.8 6.3 collective-permute-start.26
  152.2 6.3 collective-permute-start.27
  165.1 50.5 %collective-permute-start.31 = (f32[4,1,4,32]{0,3,2,1:T(8,128)S(1)}, f32[4,1,4,32]{0,3,2,1:T(8,128)S(1)}, u32[]{:S(2)}, u32[]{:S(2)}) collective-permute-start(f32[4,1,4,32]{0,3,2,1:T(8,128)S(1)} %get-tuple-element.125), channel_id=1, source_target_pairs={{0,16},{1,17},{2,18},{3,19},{4,20},{5,21},{6,22},{7,23},{8,24},{9,... | collective-permute-start | bytes 6152 | tf_op jit(solution)/shard_map/ppermute | solution.py:17
  166.8 49.0 %collective-permute-start.30 = (f32[4,1,4,32]{0,3,2,1:T(8,128)S(1)}, f32[4,1,4,32]{0,3,2,1:T(8,128)S(1)}, u32[]{:S(2)}, u32[]{:S(2)}) collective-permute-start(f32[4,1,4,32]{0,3,2,1:T(8,128)S(1)} %get-tuple-element.126), channel_id=1, source_target_pairs={{16,0},{17,1},{18,2},{19,3},{20,4},{21,5},{22,6},{23,7},{24,8},{25... | collective-permute-start | bytes 6152 | tf_op jit(solution)/shard_map/ppermute | solution.py:20
  296.0 6.7 collective-permute-start.42
  326.9 7.2 collective-permute-start.51
  328.2 7.4 collective-permute-start.50
  350.6 7.4 collective-permute-start.57
  351.9 7.5 collective-permute-start.56
  359.7 6.3 collective-permute-start.58
  395.9 6.5 collective-permute-start.63
  409.4 7.2 collective-permute-start.64
  425.8 6.6 collective-permute-start.69
  427.6 6.4 collective-permute-start.68
  451.8 6.6 collective-permute-start.75
  453.6 6.4 collective-permute-start.74
  557.0 7.2 collective-permute-start.81
  558.7 7.0 collective-permute-start.80
  581.6 6.6 collective-permute-start.87
  583.4 6.4 collective-permute-start.86
  631.8 8.4 collective-permute-start.93
  633.1 8.8 collective-permute-start.92
  655.4 8.8 collective-permute-start.99
  656.7 8.7 collective-permute-start.98
  685.3 6.3 collective-permute-start.104
  689.7 6.3 collective-permute-start.105
  697.1 6.9 collective-permute-start.106
  799.6 7.0 collective-permute-start.118
  800.9 6.4 collective-permute-start.119
  825.9 6.9 collective-permute-start.124
  846.9 7.2 collective-permute-start.129
  848.2 7.4 collective-permute-start.128
  868.8 9.1 collective-permute-start.135
  870.1 9.0 collective-permute-start.134
  914.4 6.8 collective-permute-start.141
  916.2 6.6 collective-permute-start.140
  925.7 7.2 collective-permute-start.142
  942.2 6.8 collective-permute-start.147
  944.0 6.4 collective-permute-start.146
  1007.9 6.3 collective-permute-start.153
  (128 other events, 814.1 us)
